TPU v7x, 32 devices: a whole 2x2x4 slice. The times are simulated.
32 devices in a mesh: blk: 16 (over z, x, core), rep: 2 (over y).
Axes of the slice: x: 2, y: 2, z: 4, core: 2. Of those that a mesh axis runs over, the one named last changes fastest.
Arguments:
- prices: float32 [512], replicated, may hold values from 0.5 to 1.5
- capacity: float32 [512], replicated, may hold values from -8 to 8
- coupling: bfloat16 [48, 32, 512], P(None, 'blk', 'rep'), may hold values from -0.25 to 0.25
- assign: int32 [65536], P(('blk', 'rep')), may hold values from 0 to 31
- avail: int32 [48, 65536], P(None, ('blk', 'rep')), may hold values 0 or 1
- agent_cap: float32 [65536], P(('blk', 'rep')), may hold values from 0.5 to 2
- value: float32 [48, 65536], P(None, ('blk', 'rep')), may hold values from -6 to 6
- weight: float32 [48, 65536], P(None, ('blk', 'rep')), may hold values from 0.5 to 2
- warm: float32 [48, 65536], P(None, ('blk', 'rep')), may hold values from 0 to 2
Outputs:
- plan: float32 [48, 65536], P(None, ('blk', 'rep'))
- new_prices: float32 [512], replicated
All inputs are finite; a program needn't handle non-finite values. No bound on the sum of `avail` on one device may be relied on, other than what follows from the above.
Results may differ from a plain program's by a relative error of at most 0.0003.
Values may be sent and summed in bfloat16 or wider, within the bound.
A program may use at most 64 MiB of HBM per device.

v0:
```python
import jax
import jax.numpy as jnp
from jax import lax
from jax.sharding import PartitionSpec as P

INNER = 8


def smooth_of(plan_now):
    diffs = plan_now[1:] - plan_now[:-1]
    zero_row = jnp.zeros((1, plan_now.shape[1]), jnp.float32)
    return jnp.concatenate([zero_row, diffs], 0) - jnp.concatenate([diffs, zero_row], 0)


def price_block(slab_part, lam_half):
    return jnp.einsum(
        "tfr,r->tf", slab_part.astype(jnp.float32), lam_half, precision=lax.Precision.HIGHEST
    )


def sum_block(slab_part, load_part):
    return jnp.einsum(
        "tfr,tf->r", slab_part.astype(jnp.float32), load_part, precision=lax.Precision.HIGHEST
    )


def shards(prices, capacity, coupling, assign, avail, agent_cap, value, weight, warm):
    feed_local = coupling.shape[1]
    half_rows = coupling.shape[2]
    feeders = feed_local * lax.axis_size("blk")
    total_agents = warm.shape[1] * lax.axis_size("blk") * lax.axis_size("rep")
    row_start = lax.axis_index("rep") * half_rows
    lam_half = lax.dynamic_slice_in_dim(prices, row_start, half_rows, 0)
    onehot = (assign[None, :] == lax.iota(jnp.int32, feeders)[:, None]).astype(jnp.float32)
    half_table = price_block(lax.all_gather(coupling, "blk", axis=1, tiled=True), lam_half)
    table = lax.psum(half_table, "rep")
    price = jnp.dot(table, onehot, precision=lax.Precision.HIGHEST)
    upper = agent_cap[None, :] * avail.astype(jnp.float32)
    plan = jnp.clip(warm, 0.0, upper)
    for _ in range(INNER):
        gradient = weight * plan + 1.0 * smooth_of(plan) - value + price
        plan = jnp.clip(plan - 0.15 * gradient, 0.0, upper)
    local_loads = lax.dot_general(
        plan, onehot, (((1,), (1,)), ((), ())), precision=lax.Precision.HIGHEST
    )
    local_loads = local_loads * (feeders / total_agents)
    pair_loads = lax.psum(local_loads.astype(jnp.bfloat16), "rep").astype(jnp.float32)
    half_sums = sum_block(lax.all_gather(coupling, "blk", axis=1, tiled=True), pair_loads)
    placed = lax.dynamic_update_slice_in_dim(
        jnp.zeros(prices.shape, jnp.float32), half_sums, row_start, 0
    )
    sums = lax.psum(placed, ("blk", "rep"))
    new_prices = jnp.maximum(0.0, prices + 0.1 * (sums - capacity))
    return (plan, new_prices)


def solution(mesh):
    placed = (
        P(),
        P(),
        P(None, "blk", "rep"),
        P(("blk", "rep")),
        P(None, ("blk", "rep")),
        P(("blk", "rep")),
        P(None, ("blk", "rep")),
        P(None, ("blk", "rep")),
        P(None, ("blk", "rep")),
    )
    return jax.shard_map(
        shards,
        mesh=mesh,
        in_specs=placed,
        out_specs=(P(None, ("blk", "rep")), P()),
        check_vma=False,
    )
```

profile of v0, /device:TPU:0, one launch (start us, length us, event | category | flops | bytes accessed | tf_op | source)
XLA Modules:
  0.0 86.7 jit_solution(13477924110720840931)
XLA Ops:
  0.6 0.7 copy-done.7
  1.3 0.1 dynamic_slice.3
  1.4 0.8 copy.11
  2.2 25.4 %all_gather.4 = bf16[48,32,256]{2,0,1:T(8,128)(2,1)S(1)} all-gather(bf16[48,2,256]{2,0,1:T(8,128)(2,1)S(1)} %copy.11), channel_id=1, replica_groups=mesh['blk'=16,'rep'=2] {'blk'}, dimensions={1}, use_global_device_ids=true | all-gather | bytes 835584 | tf_op jit(solution)/shard_map/all_gather | solution.py:35
  27.6 1.2 %fusion.4 = f32[1,48,32]{1,0,2:T(1,128)S(1)} fusion(f32[256,1,1]{0,1,2:T(1,128)S(1)} %bitcast.12, bf16[48,32,256]{2,0,1:T(8,128)(2,1)S(1)} %all_gather.4), kind=kOutput, calls=%fused_computation.25 | convolution fusion | flops 4718592 | bytes 793600 | tf_op jit(solution)/shard_map/tfr,r->tf/dot_general | solution.py:16
  28.8 0.1 copy.12
  28.9 8.5 %psum.21 = f32[48,32]{1,0:T(8,128)S(1)} all-reduce(f32[48,32]{1,0:T(8,128)S(1)} %bitcast.10), channel_id=1, replica_groups=mesh['blk'=16,'rep'=2] {'rep'}, use_global_device_ids=true, to_apply=%region_0.0 | all-reduce | flops 1536 | bytes 12288 | tf_op jit(solution)/shard_map/psum | solution.py:36
  37.5 0.9 %copy-done.1 = f32[48,2048]{1,0:T(8,128)S(1)} copy-done((f32[48,2048]{1,0:T(8,128)S(1)}, f32[48,2048]{1,0:T(8,128)}, u32[]{:S(2)}) %copy-start.1) | copy-done | bytes 393240
  38.5 0.1 copy-done.2
  38.6 0.5 maximum_minimum_fusion.7
  39.1 0.2 maximum_minimum_fusion.6
  39.4 0.3 maximum_minimum_fusion.5
  39.8 0.2 maximum_minimum_fusion.4
  40.0 0.3 maximum_minimum_fusion.3
  40.4 0.2 maximum_minimum_fusion.2
  40.6 0.3 maximum_minimum_fusion.1
  41.0 0.2 maximum_minimum_fusion
  41.3 0.3 fusion
  41.6 7.1 %psum.22 = bf16[48,32]{1,0:T(8,128)(2,1)S(1)} all-reduce(bf16[48,32]{1,0:T(8,128)(2,1)S(1)} %fusion), channel_id=1, replica_groups=mesh['blk'=16,'rep'=2] {'rep'}, use_global_device_ids=true, to_apply=%region_1.2 | all-reduce | flops 1536 | bytes 6144 | tf_op jit(solution)/shard_map/psum | solution.py:47
  48.7 0.1 copy.13
  48.8 0.3 fusion.5
  49.1 0.2 dynamic_update_slice.3
  49.3 36.8 %psum.23 = f32[512]{0:T(512)S(1)} all-reduce(f32[512]{0:T(512)S(1)} %dynamic_update_slice.3), channel_id=1, replica_groups=mesh['blk'=16,'rep'=2] {'blk','rep'}, use_global_device_ids=true, to_apply=%region_2.3 | all-reduce | flops 512 | bytes 4096 | tf_op jit(solution)/shard_map/psum | solution.py:52
  86.1 0.6 add_maximum_fusion
  (25 shorter events, 0.4 us)
Async XLA Ops:
  0.6 0.7 copy-start.7
  27.6 9.7 %copy-start = (s32[48,2048]{1,0:T(8,128)S(1)}, s32[48,2048]{1,0:T(8,128)}, u32[]{:S(2)}) copy-start(s32[48,2048]{1,0:T(8,128)} %param.13) | copy-start | bytes 1179652
  27.6 9.8 %copy-start.4 = (f32[48,2048]{1,0:T(8,128)S(1)}, f32[48,2048]{1,0:T(8,128)}, u32[]{:S(2)}) copy-start(f32[48,2048]{1,0:T(8,128)} %param.17) | copy-start | bytes 1179652
  28.9 8.5 %copy-start.5 = (f32[2048]{0:T(1024)S(1)}, f32[2048]{0:T(1024)}, u32[]{:S(2)}) copy-start(f32[2048]{0:T(1024)} %param.14) | copy-start | bytes 24580
  37.5 1.0 %copy-start.1 = (f32[48,2048]{1,0:T(8,128)S(1)}, f32[48,2048]{1,0:T(8,128)}, u32[]{:S(2)}) copy-start(f32[48,2048]{1,0:T(8,128)} %param.15) | copy-start | bytes 1179652
  37.5 1.1 %copy-start.2 = (f32[48,2048]{1,0:T(8,128)S(1)}, f32[48,2048]{1,0:T(8,128)}, u32[]{:S(2)}) copy-start(f32[48,2048]{1,0:T(8,128)} %param.16) | copy-start | bytes 1179652
  37.5 1.1 %copy-start.6 = (s32[2048]{0:T(1024)S(1)}, s32[2048]{0:T(1024)}, u32[]{:S(2)}) copy-start(s32[2048]{0:T(1024)} %param.12) | copy-start | bytes 24580
  41.2 7.8 %copy-start.3 = (f32[48,2048]{1,0:T(8,128)}, f32[48,2048]{1,0:T(8,128)S(1)}, u32[]{:S(2)}) copy-start(f32[48,2048]{1,0:T(8,128)S(1)} %maximum_minimum_fusion) | copy-start | bytes 1179652
  49.3 36.8 %copy-start.8 = (f32[512]{0:T(512)S(1)}, f32[512]{0:T(512)}, u32[]{:S(2)}) copy-start(f32[512]{0:T(512)} %param.10) | copy-start | bytes 6148
where the time goes:
time: 87.7 us; the launch traced here: 86.7 us
  blocking collectives  77.8 us (89%)
  local copies, waits for them, and re-layouts  3.02 us (3%)
  other arithmetic  2.8 us (3%)
  matrix products  2.29 us (3%)
    psum x1, blocking collectives, shards(): sums = lax.psum(placed, ('blk', 'rep'))  36.8 us
    all_gather x1, blocking collectives, shards(): lax.all_gather(coupling, 'blk', axis=1, tiled=True)  25.4 us
    psum x1, blocking collectives, shards(): table = lax.psum(half_table, 'rep')  8.45 us
    psum x1, blocking collectives, shards(): lax.psum(local_loads.astype(jnp.bfloat16), 'rep').astype(jnp.float32)  7.09 us
    unnamed x19, local copies, waits for them, and re-layouts  2.55 us
    min x7, other arithmetic, shards(): plan = jnp.clip(plan - 0.15 * gradient, 0.0, upper)  1.82 us

commit v1 on v0

v1 whole, which is shorter than its diff:
```python
import functools

import jax
import jax.numpy as jnp
from jax import lax
from jax.experimental import pallas as pl
from jax.experimental.pallas import tpu as pltpu
from jax.sharding import PartitionSpec as P

INNER = 8
STEP = 0.15
LANES = 128
BF16 = jnp.bfloat16
F32 = jnp.float32
MESH = pl.DeviceIdType.MESH


def three_rows(row):
    high = row.astype(BF16).astype(F32)
    rest = row - high
    mid = rest.astype(BF16).astype(F32)
    low = rest - mid
    zeros = jnp.zeros((5, row.shape[1]), F32)
    return jnp.concatenate([high, mid, low, zeros], 0).astype(BF16)


def pad_lanes(rows, width):
    if rows.shape[1] == width:
        return rows
    return jnp.concatenate(
        [rows, jnp.zeros((rows.shape[0], width - rows.shape[1]), F32)], 1
    )


def each_peer(blks, reps, my_blk, my_rep, action):
    if blks * reps <= 64:
        for db in range(blks):
            for dr in range(reps):
                if db or dr:
                    action(lax.rem(my_blk + db, blks), lax.rem(my_rep + dr, reps))
        return

    def one(k, _):
        action(lax.rem(my_blk + k // reps, blks), lax.rem(my_rep + k % reps, reps))
        return 0

    lax.fori_loop(1, blks * reps, one, 0)


def kernel(
    blks, reps, scale,
    prices_ref, capacity_ref, coup_ref, assign_ref, cap_ref, avail_hbm, value_hbm, weight_hbm, warm_hbm,
    plan_hbm, new_ref,
    avail, value, weight, warm, price, plan, split, onehot, coup,
    send_a, recv_a, send_b, recv_b, send_c, recv_c,
    in_sem, out_sem, send_sem, recv_sem,
):
    horizon, agents = warm.shape
    feed_local = coup_ref.shape[1]
    feeders = feed_local * blks
    half = coup_ref.shape[2]
    chunks = half // LANES
    my_blk, my_rep = lax.axis_index("blk"), lax.axis_index("rep")
    wide = send_a.shape[1]

    barrier = pltpu.get_barrier_semaphore()
    each_peer(
        blks, reps, my_blk, my_rep,
        lambda b, r: pl.semaphore_signal(
            barrier, inc=1, device_id={"blk": b, "rep": r}, device_id_type=MESH
        ),
    )
    fetches = [
        pltpu.make_async_copy(src, dst, in_sem.at[i])
        for i, (src, dst) in enumerate(
            ((warm_hbm, warm), (weight_hbm, weight), (value_hbm, value), (avail_hbm, avail))
        )
    ]
    for fetch in fetches:
        fetch.start()

    my_prices = prices_ref[pl.ds(my_rep * chunks, chunks), :]
    my_row = jnp.concatenate([my_prices[c : c + 1] for c in range(chunks)], 1)
    price_rows = three_rows(my_row)
    for j in range(feed_local):
        coup[j] = coup_ref[:, j, :]
        part = lax.dot_general(
            price_rows, coup[j], (((1,), (1,)), ((), ())), preferred_element_type=F32
        )
        send_a[j : j + 1, :] = pad_lanes(jnp.sum(part, 0, keepdims=True), wide)

    pl.semaphore_wait(barrier, blks * reps - 1)

    def exchange(phase, source_of, received):
        def start(b, r):
            pltpu.make_async_remote_copy(
                src_ref=source_of(b),
                dst_ref=received.at[my_rep * blks + my_blk],
                send_sem=send_sem.at[phase],
                recv_sem=recv_sem.at[phase],
                device_id={"blk": b, "rep": r},
                device_id_type=MESH,
            ).start()

        each_peer(blks, reps, my_blk, my_rep, start)

    def arrived(phase, received):
        others = received.at[pl.ds(0, blks * reps - 1)]
        pltpu.make_async_copy(others, others, recv_sem.at[phase]).wait()

    def left(phase, received):
        others = received.at[pl.ds(0, blks * reps - 1)]
        pltpu.make_async_copy(others, others, send_sem.at[phase]).wait()

    exchange(0, lambda b: send_a, recv_a)
    recv_a[my_rep * blks + my_blk] = send_a[...]

    row = lax.broadcasted_iota(jnp.int32, (feeders, agents), 0)
    feeder = lax.rem(row, blks) * feed_local + row // blks
    hot = jnp.where(feeder == assign_ref[...], 1.0, 0.0).astype(BF16)
    for part in range(3):
        onehot[part * feeders : (part + 1) * feeders, :] = hot
    for fetch in fetches:
        fetch.wait()

    arrived(0, recv_a)
    rows = []
    for j in range(feed_local):
        total = recv_a[pl.ds(0, blks), j, :]
        for r in range(1, reps):
            total = total + recv_a[pl.ds(r * blks, blks), j, :]
        rows.append(total)
    table = jnp.concatenate(rows, 0).T[:horizon]
    high = table.astype(BF16).astype(F32)
    mid = (table - high).astype(BF16).astype(F32)
    low = table - high - mid
    table3 = jnp.concatenate([high, mid, low], 1).astype(BF16)
    price[...] = jnp.dot(table3, onehot[...], preferred_element_type=F32)

    step_row = lax.broadcasted_iota(jnp.int32, (horizon, LANES), 0)
    ends = jnp.where((step_row == 0) | (step_row == horizon - 1), 1.0, 2.0)
    zero_row = jnp.zeros((1, LANES), F32)
    for c in range(agents // LANES):
        at = pl.ds(c * LANES, LANES)
        upper = cap_ref[:, at] * avail[:, at].astype(F32)
        now = jnp.clip(warm[:, at], 0.0, upper)
        keep = 1.0 - STEP * (weight[:, at] + ends)
        push = STEP * (value[:, at] - price[:, at])
        for _ in range(INNER):
            near = jnp.concatenate([zero_row, now[:-1]], 0) + jnp.concatenate([now[1:], zero_row], 0)
            now = jnp.clip(keep * now + (push + STEP * near), 0.0, upper)
        plan[:, at] = now
        coarse = now.astype(BF16)
        split[:horizon, at] = coarse
        split[horizon:, at] = (now - coarse.astype(F32)).astype(BF16)
    put = pltpu.make_async_copy(plan, plan_hbm, out_sem)
    put.start()

    both = lax.dot_general(
        onehot[:feeders, :], split[...], (((1,), (1,)), ((), ())), preferred_element_type=F32
    )
    loads = pad_lanes((both[:, :horizon] + both[:, horizon:]) * scale, wide)
    for j in range(feed_local):
        send_b[:, j, :] = loads[j * blks : (j + 1) * blks]
    exchange(1, lambda b: send_b.at[b], recv_b)
    recv_b[my_rep * blks + my_blk] = send_b[my_blk]
    arrived(1, recv_b)
    my_loads = jnp.sum(recv_b[...], 0)

    sums = jnp.zeros((8, half), F32)
    for j in range(feed_local):
        sums = sums + jnp.dot(
            three_rows(my_loads[j : j + 1, :horizon]), coup[j], preferred_element_type=F32
        )
    sums = jnp.sum(sums, 0, keepdims=True)
    for c in range(chunks):
        send_c[c : c + 1, :] = sums[:, c * LANES : (c + 1) * LANES]
    exchange(2, lambda b: send_c, recv_c)
    recv_c[my_rep * blks + my_blk] = send_c[...]
    arrived(2, recv_c)
    for r in range(reps):
        total = jnp.sum(recv_c[pl.ds(r * blks, blks)], 0)
        mine = pl.ds(r * chunks, chunks)
        new_ref[mine, :] = jnp.maximum(
            0.0, prices_ref[mine, :] + 0.1 * (total - capacity_ref[mine, :])
        )
    left(0, recv_a)
    left(1, recv_b)
    left(2, recv_c)
    put.wait()


def solution(mesh):
    blks, reps = mesh.shape["blk"], mesh.shape["rep"]

    def shards(prices, capacity, coupling, assign, avail, agent_cap, value, weight, warm):
        horizon, agents = warm.shape
        feed_local, half = coupling.shape[1:]
        feeders = feed_local * blks
        devices = blks * reps
        constraints = prices.shape[0]
        wide = -(-horizon // LANES) * LANES
        vmem = pl.BlockSpec(memory_space=pltpu.VMEM)
        hbm = pl.BlockSpec(memory_space=pl.ANY)
        rows = (constraints // LANES, LANES)
        plan, new_prices = pl.pallas_call(
            functools.partial(kernel, blks, reps, feeders / (agents * devices)),
            out_shape=(
                jax.ShapeDtypeStruct((horizon, agents), F32),
                jax.ShapeDtypeStruct(rows, F32),
            ),
            in_specs=[vmem] * 5 + [hbm] * 4,
            out_specs=(hbm, vmem),
            scratch_shapes=[
                pltpu.VMEM((horizon, agents), jnp.int32),
                pltpu.VMEM((horizon, agents), F32),
                pltpu.VMEM((horizon, agents), F32),
                pltpu.VMEM((horizon, agents), F32),
                pltpu.VMEM((horizon, agents), F32),
                pltpu.VMEM((horizon, agents), F32),
                pltpu.VMEM((2 * horizon, agents), BF16),
                pltpu.VMEM((3 * feeders, agents), BF16),
                pltpu.VMEM((feed_local, horizon, half), BF16),
                pltpu.VMEM((feed_local, wide), F32),
                pltpu.VMEM((devices, feed_local, wide), F32),
                pltpu.VMEM((blks, feed_local, wide), F32),
                pltpu.VMEM((devices, feed_local, wide), F32),
                pltpu.VMEM((half // LANES, LANES), F32),
                pltpu.VMEM((devices, half // LANES, LANES), F32),
                pltpu.SemaphoreType.DMA((4,)),
                pltpu.SemaphoreType.DMA,
                pltpu.SemaphoreType.DMA((3,)),
                pltpu.SemaphoreType.DMA((3,)),
            ],
            compiler_params=pltpu.CompilerParams(collective_id=0, has_side_effects=True),
        )(
            prices.reshape(rows), capacity.reshape(rows), coupling,
            assign.reshape(1, agents), agent_cap.reshape(1, agents),
            avail, value, weight, warm,
        )
        return plan, new_prices.reshape(constraints)

    placed = (
        P(),
        P(),
        P(None, "blk", "rep"),
        P(("blk", "rep")),
        P(None, ("blk", "rep")),
        P(("blk", "rep")),
        P(None, ("blk", "rep")),
        P(None, ("blk", "rep")),
        P(None, ("blk", "rep")),
    )
    return jax.shard_map(
        shards,
        mesh=mesh,
        in_specs=placed,
        out_specs=(P(None, ("blk", "rep")), P()),
        check_vma=False,
    )
```

time: 87.7 us -> 25.5 us (0.29)
  blocking collectives: 77.8 us -> 0 us
  Pallas kernels: 0 us -> 22.3 us
  other arithmetic: 2.8 us -> 0 us
  matrix products: 2.29 us -> 0 us
    psum x3 -> x0, blocking collectives: 52.4 us -> none  [the longest x1 36.8 us: shards(): sums = lax.psum(placed, ('blk', 'rep'))]
    all_gather x1 -> x0, blocking collectives: 25.4 us -> none  [shards(): lax.all_gather(coupling, 'blk', axis=1, tiled=True)]
    pallas_call x0 -> x1, Pallas kernels: none -> 22.3 us  [shards(): pl.pallas_call(functools.partial(kernel, blks, reps, feeders / (agents *...]
    dot_general x4 -> x0, matrix products: 2.29 us -> none  [the longest x1 1.21 us: price_block(): jnp.einsum('tfr,r->tf', slab_part.astype(jnp.float32), lam_half, precisio...]
    min x8 -> x0, other arithmetic: 1.87 us -> none  [the longest x7 1.82 us: shards(): plan = jnp.clip(plan - 0.15 * gradient, 0.0, upper)]
    unnamed x19 -> x4, local copies, waits for them, and re-layouts: 2.55 us -> 2.35 us
where the time goes in v1:
time: 25.5 us; the launch traced here: 25.3 us
  Pallas kernels  22.3 us (87%)
  local copies, waits for them, and re-layouts  2.35 us (9%)
  between operations  0.65 us (3%)
    pallas_call x1, Pallas kernels, shards(): pl.pallas_call(functools.partial(kernel, blks, reps, feeders / (agents *...  22.3 us
    unnamed x4, local copies, waits for them, and re-layouts  2.35 us

profile of v1, /device:TPU:0, one launch (start us, length us, event | category | flops | bytes accessed | tf_op | source)
XLA Modules:
  0.0 25.3 jit_solution(16277928938497360243)
XLA Ops:
  0.6 22.3 %shard_map.104 = (f32[48,2048]{1,0:T(8,128)}, f32[4,128]{1,0:T(4,128)}) custom-call(f32[4,128]{1,0:T(4,128)} %bitcast.7, f32[4,128]{1,0:T(4,128)} %bitcast.8, bf16[48,2,256]{2,1,0:T(2,128)(2,1)} %coup_ref.1, s32[1,2048]{1,0:T(1,128)} %bitcast.5, f32[1,2048]{1,0:T(1,128)} %bitcast.6, s32[48,2048]{1,0:T(8,128)} %avail_hbm.1, f32[48,2048]{1,0:T(8,128)} %value_hbm.1, ...), custom_call_target="tpu_custom_call" | custom-call | tf_op jit(solution)/shard_map/pallas_call | solution.py:206
  22.9 0.0 copy-start
  22.9 1.8 %copy.13 = f32[48,2048]{1,0:T(8,128)} copy(f32[48,2048]{1,0:T(8,128)} %get-tuple-element.8) | data formatting | bytes 786432
  24.7 0.0 copy-done
  24.7 0.6 %copy.14 = f32[512]{0:T(512)} copy(f32[512]{0:T(512)S(1)} %bitcast.9) | data formatting | bytes 4096
Async XLA Ops:
  22.9 1.8 %copy-start = (f32[4,128]{1,0:T(4,128)S(1)}, f32[4,128]{1,0:T(4,128)}, u32[]{:S(2)}) copy-start(f32[4,128]{1,0:T(4,128)} %get-tuple-element.5) | copy-start | bytes 6148

commit v2 on v1

v2 whole, which is shorter than its diff:
```python
import functools

import jax
import jax.numpy as jnp
from jax import lax
from jax.experimental import pallas as pl
from jax.experimental.pallas import tpu as pltpu
from jax.sharding import PartitionSpec as P

INNER = 8
STEP = 0.15
LANES = 128
BF16 = jnp.bfloat16
F32 = jnp.float32
MESH = pl.DeviceIdType.MESH


def three_rows(row):
    high = row.astype(BF16).astype(F32)
    rest = row - high
    mid = rest.astype(BF16).astype(F32)
    low = rest - mid
    zeros = jnp.zeros((5, row.shape[1]), F32)
    return jnp.concatenate([high, mid, low, zeros], 0).astype(BF16)


def pad_lanes(rows, width):
    if rows.shape[1] == width:
        return rows
    return jnp.concatenate(
        [rows, jnp.zeros((rows.shape[0], width - rows.shape[1]), F32)], 1
    )


def each_peer(blks, reps, my_blk, my_rep, action):
    if blks * reps <= 64:
        for db in range(blks):
            for dr in range(reps):
                if db or dr:
                    action(lax.rem(my_blk + db, blks), lax.rem(my_rep + dr, reps))
        return

    def one(k, _):
        action(lax.rem(my_blk + k // reps, blks), lax.rem(my_rep + k % reps, reps))
        return 0

    lax.fori_loop(1, blks * reps, one, 0)


def group_count(blks):
    return 4 if blks % 4 == 0 else 1


def kernel(
    blks, reps, scale,
    prices_hbm, capacity_hbm, coup_hbm, assign_hbm, cap_hbm, avail_hbm, value_hbm, weight_hbm, warm_hbm,
    plan, new_ref,
    prices, capacity, raw, assign, cap, avail, value, weight, warm, price, split, table_hot, load_hot, coup,
    send_a, recv_a, send_b, recv_b, send_c, recv_c,
    in_sem, send_sem, recv_sem,
):
    horizon, agents = warm.shape
    feed_local, half = raw.shape[1:]
    feeders = feed_local * blks
    chunks = half // LANES
    groups = group_count(blks)
    members = blks // groups
    held = groups * feed_local
    my_blk, my_rep = lax.axis_index("blk"), lax.axis_index("rep")
    my_group, my_member = my_blk // members, lax.rem(my_blk, members)
    me = my_rep * blks + my_blk
    wide = send_a.shape[1]

    barrier = pltpu.get_barrier_semaphore()
    each_peer(
        blks, reps, my_blk, my_rep,
        lambda b, r: pl.semaphore_signal(
            barrier, inc=1, device_id={"blk": b, "rep": r}, device_id_type=MESH
        ),
    )
    fetches = [
        pltpu.make_async_copy(src, dst, in_sem.at[i])
        for i, (src, dst) in enumerate(
            (
                (prices_hbm, prices), (coup_hbm, raw), (assign_hbm, assign), (cap_hbm, cap),
                (warm_hbm, warm), (weight_hbm, weight), (value_hbm, value), (avail_hbm, avail),
                (capacity_hbm, capacity),
            )
        )
    ]
    for fetch in fetches:
        fetch.start()
    fetches[0].wait()
    fetches[1].wait()

    my_prices = prices[pl.ds(my_rep * chunks, chunks), :]
    my_row = jnp.concatenate([my_prices[c : c + 1] for c in range(chunks)], 1)
    price_rows = three_rows(my_row)
    for j in range(feed_local):
        mine = raw[:, j, :]
        coup[my_group, j] = mine
        part = lax.dot_general(
            price_rows, mine, (((1,), (1,)), ((), ())), preferred_element_type=F32
        )
        send_a[j : j + 1, :] = pad_lanes(jnp.sum(part, 0, keepdims=True), wide)

    pl.semaphore_wait(barrier, blks * reps - 1)

    def send(phase, source, target, b, r):
        pltpu.make_async_remote_copy(
            src_ref=source,
            dst_ref=target,
            send_sem=send_sem.at[phase],
            recv_sem=recv_sem.at[phase],
            device_id={"blk": b, "rep": r},
            device_id_type=MESH,
        ).start()

    def wait_for(sem, received):
        others = received.at[pl.ds(0, received.shape[0] - 1)]
        pltpu.make_async_copy(others, others, sem).wait()

    each_peer(blks, reps, my_blk, my_rep, lambda b, r: send(0, send_a, recv_a.at[me], b, r))
    for dg in range(1, groups):
        there = lax.rem(my_group + dg, groups) * members + my_member
        send(3, coup.at[my_group], coup.at[my_group], there, my_rep)
    recv_a[me] = send_a[...]

    fetches[2].wait()
    row = lax.broadcasted_iota(jnp.int32, (feeders, agents), 0)
    feeder = lax.rem(row, blks) * feed_local + row // blks
    hot = jnp.where(feeder == assign[...], 1.0, 0.0).astype(BF16)
    for part in range(3):
        table_hot[part * feeders : (part + 1) * feeders, :] = hot
    slot = row // members
    feeder = ((slot // feed_local) * members + lax.rem(row, members)) * feed_local + lax.rem(
        slot, feed_local
    )
    load_hot[...] = jnp.where(feeder == assign[...], 1.0, 0.0).astype(BF16)
    for fetch in fetches[3:]:
        fetch.wait()

    wait_for(recv_sem.at[0], recv_a)
    rows = []
    for j in range(feed_local):
        total = recv_a[pl.ds(0, blks), j, :]
        for r in range(1, reps):
            total = total + recv_a[pl.ds(r * blks, blks), j, :]
        rows.append(total)
    table = jnp.concatenate(rows, 0).T[:horizon]
    high = table.astype(BF16).astype(F32)
    mid = (table - high).astype(BF16).astype(F32)
    low = table - high - mid
    table3 = jnp.concatenate([high, mid, low], 1).astype(BF16)
    price[...] = jnp.dot(table3, table_hot[...], preferred_element_type=F32)

    step_row = lax.broadcasted_iota(jnp.int32, (horizon, LANES), 0)
    ends = jnp.where((step_row == 0) | (step_row == horizon - 1), 1.0, 2.0)
    zero_row = jnp.zeros((1, LANES), F32)
    for c in range(agents // LANES):
        at = pl.ds(c * LANES, LANES)
        upper = cap[:, at] * avail[:, at].astype(F32)
        now = jnp.clip(warm[:, at], 0.0, upper)
        keep = 1.0 - STEP * (weight[:, at] + ends)
        push = STEP * (value[:, at] - price[:, at])
        for _ in range(INNER):
            near = jnp.concatenate([zero_row, now[:-1]], 0) + jnp.concatenate([now[1:], zero_row], 0)
            now = jnp.clip(keep * now + (push + STEP * near), 0.0, upper)
        plan[:, at] = now
        coarse = now.astype(BF16)
        split[:horizon, at] = coarse
        split[horizon:, at] = (now - coarse.astype(F32)).astype(BF16)

    both = lax.dot_general(
        load_hot[...], split[...], (((1,), (1,)), ((), ())), preferred_element_type=F32
    )
    loads = pad_lanes((both[:, :horizon] + both[:, horizon:]) * scale, wide)
    for q in range(held):
        send_b[:, q, :] = loads[q * members : (q + 1) * members]
    my_seat = my_rep * members + my_member

    def send_loads(m, r):
        send(1, send_b.at[m], recv_b.at[my_seat], my_group * members + m, r)

    each_peer(members, reps, my_member, my_rep, send_loads)
    recv_b[my_seat] = send_b[my_member]
    wait_for(recv_sem.at[1], recv_b)
    group_loads = jnp.sum(recv_b[...], 0)[:, :horizon]
    if groups > 1:
        wait_for(recv_sem.at[3], coup)

    high = group_loads.astype(BF16).astype(F32)
    mid = (group_loads - high).astype(BF16).astype(F32)
    low = group_loads - high - mid
    stack = jnp.concatenate([high, mid, low, jnp.zeros_like(low)], 0)
    owner = lax.rem(lax.broadcasted_iota(jnp.int32, stack.shape, 0), held)
    sums = jnp.zeros((4 * held, half), F32)
    for q in range(held):
        sums = sums + jnp.dot(
            jnp.where(owner == q, stack, 0.0).astype(BF16),
            coup[q // feed_local, q % feed_local],
            preferred_element_type=F32,
        )
    sums = jnp.sum(sums, 0, keepdims=True)
    for c in range(chunks):
        send_c[c : c + 1, :] = sums[:, c * LANES : (c + 1) * LANES]
    each_peer(blks, reps, my_blk, my_rep, lambda b, r: send(2, send_c, recv_c.at[me], b, r))
    recv_c[me] = send_c[...]
    wait_for(recv_sem.at[2], recv_c)
    for r in range(reps):
        total = jnp.sum(recv_c[pl.ds(r * blks, blks)], 0)
        here = pl.ds(r * chunks, chunks)
        new_ref[here, :] = jnp.maximum(
            0.0, prices[here, :] + 0.1 * (total - capacity[here, :])
        )
    wait_for(send_sem.at[0], recv_a)
    wait_for(send_sem.at[1], recv_b)
    wait_for(send_sem.at[2], recv_c)
    if groups > 1:
        wait_for(send_sem.at[3], coup)


def solution(mesh):
    blks, reps = mesh.shape["blk"], mesh.shape["rep"]
    groups = group_count(blks)
    members = blks // groups

    def shards(prices, capacity, coupling, assign, avail, agent_cap, value, weight, warm):
        horizon, agents = warm.shape
        feed_local, half = coupling.shape[1:]
        feeders = feed_local * blks
        devices = blks * reps
        constraints = prices.shape[0]
        wide = -(-horizon // LANES) * LANES
        vmem = pl.BlockSpec(memory_space=pltpu.VMEM)
        hbm = pl.BlockSpec(memory_space=pl.ANY)
        rows = (constraints // LANES, LANES)
        whole = (horizon, agents)
        plan, new_prices = pl.pallas_call(
            functools.partial(kernel, blks, reps, feeders / (agents * devices)),
            out_shape=(pltpu.VMEM(whole, F32), pltpu.VMEM(rows, F32)),
            in_specs=[hbm] * 9,
            out_specs=(vmem, vmem),
            scratch_shapes=[
                pltpu.VMEM(rows, F32),
                pltpu.VMEM(rows, F32),
                pltpu.VMEM(coupling.shape, BF16),
                pltpu.VMEM((1, agents), jnp.int32),
                pltpu.VMEM((1, agents), F32),
                pltpu.VMEM(whole, jnp.int32),
                pltpu.VMEM(whole, F32),
                pltpu.VMEM(whole, F32),
                pltpu.VMEM(whole, F32),
                pltpu.VMEM(whole, F32),
                pltpu.VMEM((2 * horizon, agents), BF16),
                pltpu.VMEM((3 * feeders, agents), BF16),
                pltpu.VMEM((feeders, agents), BF16),
                pltpu.VMEM((groups, feed_local, horizon, half), BF16),
                pltpu.VMEM((feed_local, wide), F32),
                pltpu.VMEM((devices, feed_local, wide), F32),
                pltpu.VMEM((members, groups * feed_local, wide), F32),
                pltpu.VMEM((members * reps, groups * feed_local, wide), F32),
                pltpu.VMEM((half // LANES, LANES), F32),
                pltpu.VMEM((devices, half // LANES, LANES), F32),
                pltpu.SemaphoreType.DMA((9,)),
                pltpu.SemaphoreType.DMA((4,)),
                pltpu.SemaphoreType.DMA((4,)),
            ],
            compiler_params=pltpu.CompilerParams(collective_id=0, has_side_effects=True),
        )(
            prices.reshape(rows), capacity.reshape(rows), coupling,
            assign.reshape(1, agents), agent_cap.reshape(1, agents),
            avail, value, weight, warm,
        )
        return plan, new_prices.reshape(constraints)

    placed = (
        P(),
        P(),
        P(None, "blk", "rep"),
        P(("blk", "rep")),
        P(None, ("blk", "rep")),
        P(("blk", "rep")),
        P(None, ("blk", "rep")),
        P(None, ("blk", "rep")),
        P(None, ("blk", "rep")),
    )
    return jax.shard_map(
        shards,
        mesh=mesh,
        in_specs=placed,
        out_specs=(P(None, ("blk", "rep")), P()),
        check_vma=False,
    )
```

time: 25.5 us -> 23 us (0.902)
  Pallas kernels: 22.3 us -> 20.9 us
  local copies, waits for them, and re-layouts: 2.35 us -> 1.33 us
    pallas_call x1, Pallas kernels: 22.3 us -> 20.9 us  [shards(): pl.pallas_call(functools.partial(kernel, blks, reps, feeders / (agents *...]
    unnamed x4 -> x2, local copies, waits for them, and re-layouts: 2.35 us -> 1.33 us
where the time goes in v2:
time: 23 us; the launch traced here: 22.8 us
  Pallas kernels  20.9 us (91%)
  local copies, waits for them, and re-layouts  1.33 us (6%)
  between operations  0.64 us (3%)
    pallas_call x1, Pallas kernels, shards(): pl.pallas_call(functools.partial(kernel, blks, reps, feeders / (agents *...  20.9 us
    unnamed x2, local copies, waits for them, and re-layouts  1.33 us

profile of v2, /device:TPU:0, one launch (start us, length us, event | category | flops | bytes accessed | tf_op | source)
XLA Modules:
  0.0 22.8 jit_solution(2362028653205989735)
XLA Ops:
  0.6 20.9 %shard_map.104 = (f32[48,2048]{1,0:T(8,128)S(1)}, f32[4,128]{1,0:T(4,128)S(1)}) custom-call(f32[4,128]{1,0:T(4,128)} %bitcast.8, f32[4,128]{1,0:T(4,128)} %bitcast.9, bf16[48,2,256]{2,1,0:T(2,128)(2,1)} %coup_hbm.1, s32[1,2048]{1,0:T(1,128)} %bitcast.6, f32[1,2048]{1,0:T(1,128)} %bitcast.7, s32[48,2048]{1,0:T(8,128)} %avail_hbm.1, f32[48,2048]{1,0:T(8,128)} %value_hbm.1, ...), custom_call_target="tpu_custom_call" | custom-call | tf_op jit(solution)/shard_map/pallas_call | solution.py:239
  21.5 0.7 %copy.13 = f32[48,2048]{1,0:T(8,128)} copy(f32[48,2048]{1,0:T(8,128)S(1)} %get-tuple-element.6) | data formatting | bytes 786432
  22.3 0.6 %copy.14 = f32[512]{0:T(512)} copy(f32[512]{0:T(512)S(1)} %bitcast.5) | data formatting | bytes 4096

commit v3 on v2

--- a/solution.py
+++ b/solution.py
@@ -10,6 +10,8 @@
 INNER = 8
 STEP = 0.15
 LANES = 128
+BLOCK = 256
+EIGHT = 8
 BF16 = jnp.bfloat16
 F32 = jnp.float32
 MESH = pl.DeviceIdType.MESH
@@ -55,13 +57,15 @@
     blks, reps, scale,
     prices_hbm, capacity_hbm, coup_hbm, assign_hbm, cap_hbm, avail_hbm, value_hbm, weight_hbm, warm_hbm,
     plan, new_ref,
-    prices, capacity, raw, assign, cap, avail, value, weight, warm, price, split, table_hot, load_hot, coup,
+    prices, capacity, raw, stage, assign, cap, avail, value, weight, warm, start, upper, keep, push, done, table_hot, load_hot, coup,
     send_a, recv_a, send_b, recv_b, send_c, recv_c,
-    in_sem, send_sem, recv_sem,
+    in_sem, out_sem, send_sem, recv_sem,
 ):
-    horizon, agents = warm.shape
+    blocks, horizon = warm.shape[:2]
+    agents = blocks * LANES
     feed_local, half = raw.shape[1:]
     feeders = feed_local * blks
+    strides = horizon // EIGHT
     chunks = half // LANES
     groups = group_count(blks)
     members = blks // groups
@@ -83,13 +87,18 @@
         for i, (src, dst) in enumerate(
             (
                 (prices_hbm, prices), (coup_hbm, raw), (assign_hbm, assign), (cap_hbm, cap),
-                (warm_hbm, warm), (weight_hbm, weight), (value_hbm, value), (avail_hbm, avail),
                 (capacity_hbm, capacity),
             )
         )
     ]
     for fetch in fetches:
         fetch.start()
+    tiled = ((warm_hbm, warm), (weight_hbm, weight), (value_hbm, value), (avail_hbm, avail))
+    for i, (src, dst) in enumerate(tiled):
+        for c in range(agents // LANES):
+            pltpu.make_async_copy(
+                src.at[:, pl.ds(c * LANES, LANES)], dst.at[c], in_sem.at[5 + i]
+            ).start()
     fetches[0].wait()
     fetches[1].wait()
 
@@ -97,7 +106,18 @@
     my_row = jnp.concatenate([my_prices[c : c + 1] for c in range(chunks)], 1)
     price_rows = three_rows(my_row)
     for j in range(feed_local):
-        mine = raw[:, j, :]
+        natural = raw[:, j, :].astype(F32)
+        for c in range(chunks):
+            stage[c] = natural[:, c * LANES : (c + 1) * LANES]
+        mine = jnp.concatenate(
+            [
+                jnp.concatenate(
+                    [stage[c, pl.ds(v, EIGHT, stride=strides), :] for v in range(strides)], 0
+                )
+                for c in range(chunks)
+            ],
+            1,
+        ).astype(BF16)
         coup[my_group, j] = mine
         part = lax.dot_general(
             price_rows, mine, (((1,), (1,)), ((), ())), preferred_element_type=F32
@@ -139,6 +159,26 @@
     load_hot[...] = jnp.where(feeder == assign[...], 1.0, 0.0).astype(BF16)
     for fetch in fetches[3:]:
         fetch.wait()
+    for i, (_, dst) in enumerate(tiled):
+        pltpu.make_async_copy(dst, dst, in_sem.at[5 + i]).wait()
+
+    eighth = lax.broadcasted_iota(jnp.int32, (EIGHT, LANES), 0)
+    first, last = eighth == 0, eighth == EIGHT - 1
+    for c in range(agents // LANES):
+        at = pl.ds(c * LANES, LANES)
+        for v in range(strides):
+            there = pl.ds(v, EIGHT, stride=strides)
+            here = pl.ds(v * EIGHT, EIGHT)
+            limit = cap[:, at] * avail[c, there, :].astype(F32)
+            near = jnp.full((EIGHT, LANES), 2.0, F32)
+            if v == 0:
+                near = near - jnp.where(first, 1.0, 0.0)
+            if v == strides - 1:
+                near = near - jnp.where(last, 1.0, 0.0)
+            upper[here, at] = limit
+            start[here, at] = jnp.clip(warm[c, there, :], 0.0, limit)
+            keep[here, at] = 1.0 - STEP * (weight[c, there, :] + near)
+            push[here, at] = STEP * value[c, there, :]
 
     wait_for(recv_sem.at[0], recv_a)
     rows = []
@@ -152,28 +192,43 @@
     mid = (table - high).astype(BF16).astype(F32)
     low = table - high - mid
     table3 = jnp.concatenate([high, mid, low], 1).astype(BF16)
-    price[...] = jnp.dot(table3, table_hot[...], preferred_element_type=F32)
-
-    step_row = lax.broadcasted_iota(jnp.int32, (horizon, LANES), 0)
-    ends = jnp.where((step_row == 0) | (step_row == horizon - 1), 1.0, 2.0)
-    zero_row = jnp.zeros((1, LANES), F32)
-    for c in range(agents // LANES):
-        at = pl.ds(c * LANES, LANES)
-        upper = cap[:, at] * avail[:, at].astype(F32)
-        now = jnp.clip(warm[:, at], 0.0, upper)
-        keep = 1.0 - STEP * (weight[:, at] + ends)
-        push = STEP * (value[:, at] - price[:, at])
-        for _ in range(INNER):
-            near = jnp.concatenate([zero_row, now[:-1]], 0) + jnp.concatenate([now[1:], zero_row], 0)
-            now = jnp.clip(keep * now + (push + STEP * near), 0.0, upper)
-        plan[:, at] = now
-        coarse = now.astype(BF16)
-        split[:horizon, at] = coarse
-        split[horizon:, at] = (now - coarse.astype(F32)).astype(BF16)
-
-    both = lax.dot_general(
-        load_hot[...], split[...], (((1,), (1,)), ((), ())), preferred_element_type=F32
-    )
+
+    both = jnp.zeros((feeders, 2 * horizon), F32)
+    for c in range(agents // BLOCK):
+        block = pl.ds(c * BLOCK, BLOCK)
+        price = STEP * jnp.dot(table3, table_hot[:, block], preferred_element_type=F32)
+        parts = []
+        for d in range(BLOCK // LANES):
+            at = pl.ds(c * BLOCK + d * LANES, LANES)
+            rows = [slice(v * EIGHT, (v + 1) * EIGHT) for v in range(strides)]
+            now = [start[row, at] for row in rows]
+            most = [upper[row, at] for row in rows]
+            held_back = [keep[row, at] for row in rows]
+            drive = [
+                push[row, at] - price[row, d * LANES : (d + 1) * LANES] for row in rows
+            ]
+            for _ in range(INNER):
+                before = jnp.where(first, 0.0, pltpu.roll(now[-1], 1, 0))
+                after = jnp.where(last, 0.0, pltpu.roll(now[0], EIGHT - 1, 0))
+                line = [before] + now + [after]
+                now = [
+                    jnp.clip(
+                        held_back[v] * now[v] + (drive[v] + STEP * (line[v] + line[v + 2])),
+                        0.0, most[v],
+                    )
+                    for v in range(strides)
+                ]
+            for v in range(strides):
+                done[c * (BLOCK // LANES) + d, pl.ds(v, EIGHT, stride=strides), :] = now[v]
+            now = jnp.concatenate(now, 0)
+            coarse = now.astype(BF16).astype(F32)
+            parts.append(jnp.concatenate([coarse, now - coarse], 0).astype(BF16))
+        both = both + lax.dot_general(
+            load_hot[:, block], jnp.concatenate(parts, 1), (((1,), (1,)), ((), ())),
+            preferred_element_type=F32,
+        )
+    for c in range(blocks):
+        pltpu.make_async_copy(done.at[c], plan.at[:, pl.ds(c * LANES, LANES)], out_sem).start()
     loads = pad_lanes((both[:, :horizon] + both[:, horizon:]) * scale, wide)
     for q in range(held):
         send_b[:, q, :] = loads[q * members : (q + 1) * members]
@@ -213,6 +268,7 @@
         new_ref[here, :] = jnp.maximum(
             0.0, prices[here, :] + 0.1 * (total - capacity[here, :])
         )
+    pltpu.make_async_copy(done, done, out_sem).wait()
     wait_for(send_sem.at[0], recv_a)
     wait_for(send_sem.at[1], recv_b)
     wait_for(send_sem.at[2], recv_c)
@@ -236,6 +292,7 @@
         hbm = pl.BlockSpec(memory_space=pl.ANY)
         rows = (constraints // LANES, LANES)
         whole = (horizon, agents)
+        tiles = (agents // LANES, horizon, LANES)
         plan, new_prices = pl.pallas_call(
             functools.partial(kernel, blks, reps, feeders / (agents * devices)),
             out_shape=(pltpu.VMEM(whole, F32), pltpu.VMEM(rows, F32)),
@@ -245,14 +302,18 @@
                 pltpu.VMEM(rows, F32),
                 pltpu.VMEM(rows, F32),
                 pltpu.VMEM(coupling.shape, BF16),
+                pltpu.VMEM((half // LANES, horizon, LANES), F32),
                 pltpu.VMEM((1, agents), jnp.int32),
                 pltpu.VMEM((1, agents), F32),
-                pltpu.VMEM(whole, jnp.int32),
+                pltpu.VMEM(tiles, jnp.int32),
+                pltpu.VMEM(tiles, F32),
+                pltpu.VMEM(tiles, F32),
+                pltpu.VMEM(tiles, F32),
                 pltpu.VMEM(whole, F32),
                 pltpu.VMEM(whole, F32),
                 pltpu.VMEM(whole, F32),
                 pltpu.VMEM(whole, F32),
-                pltpu.VMEM((2 * horizon, agents), BF16),
+                pltpu.VMEM(tiles, F32),
                 pltpu.VMEM((3 * feeders, agents), BF16),
                 pltpu.VMEM((feeders, agents), BF16),
                 pltpu.VMEM((groups, feed_local, horizon, half), BF16),
@@ -263,6 +324,7 @@
                 pltpu.VMEM((half // LANES, LANES), F32),
                 pltpu.VMEM((devices, half // LANES, LANES), F32),
                 pltpu.SemaphoreType.DMA((9,)),
+                pltpu.SemaphoreType.DMA,
                 pltpu.SemaphoreType.DMA((4,)),
                 pltpu.SemaphoreType.DMA((4,)),
             ],

time: 23 us -> 22.6 us (0.983)
  Pallas kernels: 20.9 us -> 20.5 us
    pallas_call x1, Pallas kernels: 20.9 us -> 20.5 us  [shards(): pl.pallas_call(functools.partial(kernel, blks, reps, feeders / (agents *...]
where the time goes in v3:
time: 22.6 us; the launch traced here: 22.4 us
  Pallas kernels  20.5 us (91%)
  local copies, waits for them, and re-layouts  1.33 us (6%)
  between operations  0.64 us (3%)
    pallas_call x1, Pallas kernels, shards(): pl.pallas_call(functools.partial(kernel, blks, reps, feeders / (agents *...  20.5 us
    unnamed x2, local copies, waits for them, and re-layouts  1.33 us

profile of v3, /device:TPU:0, one launch (start us, length us, event | category | flops | bytes accessed | tf_op | source)
XLA Modules:
  0.0 22.4 jit_solution(16618282662954931498)
XLA Ops:
  0.6 20.5 %shard_map.104 = (f32[48,2048]{1,0:T(8,128)S(1)}, f32[4,128]{1,0:T(4,128)S(1)}) custom-call(f32[4,128]{1,0:T(4,128)} %bitcast.8, f32[4,128]{1,0:T(4,128)} %bitcast.9, bf16[48,2,256]{2,1,0:T(2,128)(2,1)} %coup_hbm.1, s32[1,2048]{1,0:T(1,128)} %bitcast.6, f32[1,2048]{1,0:T(1,128)} %bitcast.7, s32[48,2048]{1,0:T(8,128)} %avail_hbm.1, f32[48,2048]{1,0:T(8,128)} %value_hbm.1, ...), custom_call_target="tpu_custom_call" | custom-call | tf_op jit(solution)/shard_map/pallas_call | solution.py:296
  21.1 0.7 %copy.13 = f32[48,2048]{1,0:T(8,128)} copy(f32[48,2048]{1,0:T(8,128)S(1)} %get-tuple-element.6) | data formatting | bytes 786432
  21.9 0.6 %copy.14 = f32[512]{0:T(512)} copy(f32[512]{0:T(512)S(1)} %bitcast.5) | data formatting | bytes 4096

commit v4 on v3

--- a/solution.py
+++ b/solution.py
@@ -36,10 +36,18 @@
 
 def each_peer(blks, reps, my_blk, my_rep, action):
     if blks * reps <= 64:
-        for db in range(blks):
-            for dr in range(reps):
-                if db or dr:
-                    action(lax.rem(my_blk + db, blks), lax.rem(my_rep + dr, reps))
+        groups = group_count(blks)
+        members = blks // groups
+        my_group, my_member = my_blk // members, lax.rem(my_blk, members)
+        far_first = sorted(range(groups), key=lambda dg: (dg == 0, -abs(2 * dg - groups)))
+        for dg in far_first:
+            group = lax.rem(my_group + dg, groups) * members
+            for dm in reversed(range(members)):
+                for dr in reversed(range(reps)):
+                    if dg or dm or dr:
+                        action(
+                            group + lax.rem(my_member + dm, members), lax.rem(my_rep + dr, reps)
+                        )
         return
 
     def one(k, _):

time: 22.6 us -> 22.5 us (level)
  no operation moved by 1% of the time
where the time goes in v4:
time: 22.5 us; the launch traced here: 22.3 us
  Pallas kernels  20.4 us (91%)
  local copies, waits for them, and re-layouts  1.33 us (6%)
  between operations  0.64 us (3%)
    pallas_call x1, Pallas kernels, shards(): pl.pallas_call(functools.partial(kernel, blks, reps, feeders / (agents *...  20.4 us
    unnamed x2, local copies, waits for them, and re-layouts  1.33 us

profile of v4, /device:TPU:0, one launch (start us, length us, event | category | flops | bytes accessed | tf_op | source)
XLA Modules:
  0.0 22.3 jit_solution(11703419559313698642)
XLA Ops:
  0.6 20.4 %shard_map.104 = (f32[48,2048]{1,0:T(8,128)S(1)}, f32[4,128]{1,0:T(4,128)S(1)}) custom-call(f32[4,128]{1,0:T(4,128)} %bitcast.8, f32[4,128]{1,0:T(4,128)} %bitcast.9, bf16[48,2,256]{2,1,0:T(2,128)(2,1)} %coup_hbm.1, s32[1,2048]{1,0:T(1,128)} %bitcast.6, f32[1,2048]{1,0:T(1,128)} %bitcast.7, s32[48,2048]{1,0:T(8,128)} %avail_hbm.1, f32[48,2048]{1,0:T(8,128)} %value_hbm.1, ...), custom_call_target="tpu_custom_call" | custom-call | tf_op jit(solution)/shard_map/pallas_call | solution.py:304
  21.0 0.7 %copy.13 = f32[48,2048]{1,0:T(8,128)} copy(f32[48,2048]{1,0:T(8,128)S(1)} %get-tuple-element.6) | data formatting | bytes 786432
  21.8 0.6 %copy.14 = f32[512]{0:T(512)} copy(f32[512]{0:T(512)S(1)} %bitcast.5) | data formatting | bytes 4096

commit v5 on v4

--- a/solution.py
+++ b/solution.py
@@ -149,9 +149,6 @@
         pltpu.make_async_copy(others, others, sem).wait()
 
     each_peer(blks, reps, my_blk, my_rep, lambda b, r: send(0, send_a, recv_a.at[me], b, r))
-    for dg in range(1, groups):
-        there = lax.rem(my_group + dg, groups) * members + my_member
-        send(3, coup.at[my_group], coup.at[my_group], there, my_rep)
     recv_a[me] = send_a[...]
 
     fetches[2].wait()
@@ -189,6 +186,9 @@
             push[here, at] = STEP * value[c, there, :]
 
     wait_for(recv_sem.at[0], recv_a)
+    for dg in range(1, groups):
+        there = lax.rem(my_group + dg, groups) * members + my_member
+        send(3, coup.at[my_group], coup.at[my_group], there, my_rep)
     rows = []
     for j in range(feed_local):
         total = recv_a[pl.ds(0, blks), j, :]

time: 22.5 us -> 23.8 us (1.058)
  Pallas kernels: 20.4 us -> 21.6 us
    pallas_call x1, Pallas kernels: 20.4 us -> 21.6 us  [shards(): pl.pallas_call(functools.partial(kernel, blks, reps, feeders / (agents *...]
where the time goes in v5:
time: 23.8 us; the launch traced here: 23.6 us
  Pallas kernels  21.6 us (91%)
  local copies, waits for them, and re-layouts  1.33 us (6%)
  between operations  0.64 us (3%)
    pallas_call x1, Pallas kernels, shards(): pl.pallas_call(functools.partial(kernel, blks, reps, feeders / (agents *...  21.6 us
    unnamed x2, local copies, waits for them, and re-layouts  1.33 us

profile of v5, /device:TPU:0, one launch (start us, length us, event | category | flops | bytes accessed | tf_op | source)
XLA Modules:
  0.0 23.6 jit_solution(17133451290681746766)
XLA Ops:
  0.6 21.6 %shard_map.104 = (f32[48,2048]{1,0:T(8,128)S(1)}, f32[4,128]{1,0:T(4,128)S(1)}) custom-call(f32[4,128]{1,0:T(4,128)} %bitcast.8, f32[4,128]{1,0:T(4,128)} %bitcast.9, bf16[48,2,256]{2,1,0:T(2,128)(2,1)} %coup_hbm.1, s32[1,2048]{1,0:T(1,128)} %bitcast.6, f32[1,2048]{1,0:T(1,128)} %bitcast.7, s32[48,2048]{1,0:T(8,128)} %avail_hbm.1, f32[48,2048]{1,0:T(8,128)} %value_hbm.1, ...), custom_call_target="tpu_custom_call" | custom-call | tf_op jit(solution)/shard_map/pallas_call | solution.py:304
  22.3 0.7 %copy.13 = f32[48,2048]{1,0:T(8,128)} copy(f32[48,2048]{1,0:T(8,128)S(1)} %get-tuple-element.6) | data formatting | bytes 786432
  23.0 0.6 %copy.14 = f32[512]{0:T(512)} copy(f32[512]{0:T(512)S(1)} %bitcast.5) | data formatting | bytes 4096
